TPU v7x, 32 devices: a whole 2x2x4 slice. The times are simulated.
32 devices in a mesh: groups: 2 (over x), expert: 16 (over z, y, core).
Axes of the slice: x: 2, y: 2, z: 4, core: 2. Of those that a mesh axis runs over, the one named last changes fastest.
Arguments:
- query_features: bfloat16 [4096, 1024], P(('groups', 'expert')), parts along dimension 0, may hold values from -6 to 6
- query_job_label: int32 [4096], P(('groups', 'expert')), parts along dimension 0, may hold values from 0 to 7, as said below
- selected_specialists: int32 [4096, 2], P(('groups', 'expert')), parts along dimension 0, may hold values from 0 to 8, as said below
- whole_number_mixing_factors: int32 [4096, 2], P(('groups', 'expert')), parts along dimension 0, may hold values from 1 to 8
- copy_room_sizes: int32 [16], replicated, may hold values from 256 to 384, as said below
- first_layer_matrix: bfloat16 [16, 1024, 2048], P('expert'), as said below
- second_layer_matrix: bfloat16 [16, 2048, 1024], P('expert'), as said below
Outputs:
- mixture: bfloat16 [4096, 1024], P(('groups', 'expert')), parts along dimension 0
There are 2 independent parts, one for each index of `groups`. A program takes and returns all parts, laid end to end along the dimension named above; an argument that names none is the same for every part. Nothing has to cross between parts.
Inputs may be any that keep to these rules, and one draw needn't show every extreme that they name: `query_job_label`: each request's task number; column 0 of `selected_specialists` names a task expert of this task. `selected_specialists`: column 0 names a task expert of the row's task (number r from 8 on is task expert r - 8), column 1 a shared expert (below 8). From the rows of one device at most 32 entries go to one expert copy, and in every draw some copy receives exactly 32 entries from every device. `copy_room_sizes`: some copy has capacity 384 and some copy 2 * 128. `first_layer_matrix`: the 1 copies of one shared expert hold equal weights. `second_layer_matrix`: the 1 copies of one shared expert hold equal weights.
All inputs are finite; a program needn't handle non-finite values.
Results may differ from a plain program's by a relative error of at most 0.0058.
Values may be sent and summed in bfloat16 or wider, within the bound.
A program may use at most 64 MiB of HBM per device.

v0:
```python
import jax
import jax.numpy as jnp
from jax import lax
from jax.sharding import PartitionSpec as P

TASKS = 8
SHARED = 8


def expert_mlp(block_rows, up_matrix, down_matrix):
    hidden = jax.nn.gelu(jnp.dot(block_rows, up_matrix, preferred_element_type=jnp.float32)).astype(
        jnp.bfloat16
    )
    return jnp.dot(hidden, down_matrix, preferred_element_type=jnp.float32).astype(jnp.bfloat16)


def shards(
    query_features,
    query_job_label,
    selected_specialists,
    whole_number_mixing_factors,
    copy_room_sizes,
    first_layer_matrix,
    second_layer_matrix,
):
    specialist_networks = copy_room_sizes.shape[0]
    row_count = query_features.shape[0]
    feature_width = query_features.shape[1]
    top_count = selected_specialists.shape[1]
    copies = specialist_networks // (2 * SHARED)
    task_width = specialist_networks // (2 * TASKS)
    slot_size = 4 * row_count // specialist_networks
    up_matrix = first_layer_matrix[0]
    down_matrix = second_layer_matrix[0]
    own_index = lax.axis_index("expert")
    row_local = jnp.arange(row_count, dtype=jnp.int32)
    shared_copy = selected_specialists * copies + (row_local % copies)[:, None]
    task_copy = (
        SHARED * copies + query_job_label[:, None] * task_width + selected_specialists - SHARED
    )
    expert_ids = jnp.where(selected_specialists < SHARED, shared_copy, task_copy)
    linear_specialist_number = expert_ids.reshape(-1)
    specialist_onehot = (
        linear_specialist_number[:, None]
        == jnp.arange(specialist_networks, dtype=jnp.int32)[None, :]
    ).astype(jnp.int32)
    counts = jnp.sum(specialist_onehot, axis=0)
    local_rank = jnp.sum(
        (jnp.cumsum(specialist_onehot, axis=0) - specialist_onehot) * specialist_onehot, axis=1
    )
    all_counts = lax.all_gather(counts[None, :], "expert", axis=0, tiled=True)
    below_mask = (jnp.arange(all_counts.shape[0]) < own_index).astype(jnp.int32)
    offset = jnp.sum(all_counts * below_mask[:, None], axis=0)
    arrival_rank = local_rank + jnp.sum(specialist_onehot * offset[None, :], axis=1)
    slot_room_bounds = jnp.sum(specialist_onehot * copy_room_sizes[None, :], axis=1)
    surviving_slot_flags = arrival_rank < slot_room_bounds
    source_rows = jnp.arange(linear_specialist_number.shape[0], dtype=jnp.int32) // top_count
    send_index = jnp.where(
        surviving_slot_flags,
        linear_specialist_number * slot_size + local_rank,
        specialist_networks * slot_size,
    )
    outgoing = jnp.zeros((specialist_networks * slot_size, feature_width), jnp.bfloat16)
    outgoing = (
        outgoing.at[send_index]
        .set(query_features[source_rows], mode="drop")
        .reshape(specialist_networks, slot_size, feature_width)
    )
    arrived = lax.all_to_all(outgoing, "expert", split_axis=0, concat_axis=0, tiled=True)
    returned = lax.all_to_all(
        expert_mlp(arrived.reshape(-1, feature_width), up_matrix, down_matrix).reshape(
            arrived.shape
        ),
        "expert",
        split_axis=0,
        concat_axis=0,
        tiled=True,
    )
    read_index = jnp.where(
        surviving_slot_flags, linear_specialist_number * slot_size + local_rank, 0
    )
    picked = returned.reshape(-1, feature_width)[read_index]
    gate_float = whole_number_mixing_factors.astype(jnp.float32)
    gate_share = gate_float / jnp.sum(gate_float, axis=1, keepdims=True)
    row_weight = gate_share.reshape(-1) * surviving_slot_flags.astype(jnp.float32)
    weighted = row_weight[:, None] * picked.astype(jnp.float32)
    return jnp.sum(weighted.reshape(row_count, top_count, feature_width), axis=1).astype(
        jnp.bfloat16
    )


def solution(mesh):
    in_specs = (
        P(("groups", "expert"), None),
        P(("groups", "expert")),
        P(("groups", "expert"), None),
        P(("groups", "expert"), None),
        P(),
        P("expert", None, None),
        P("expert", None, None),
    )
    out_specs = P(("groups", "expert"), None)
    return jax.shard_map(shards, mesh=mesh, in_specs=in_specs, out_specs=out_specs, check_vma=False)
```

profile of v0, /device:TPU:9, one launch (start us, length us, event | category | flops | bytes accessed | tf_op | source)
XLA Modules:
  0.0 92.8 jit_solution(5855867571831604541)
XLA Ops:
  0.0 0.0 copy-start
  0.0 0.7 broadcast_add_fusion
  0.7 0.7 broadcast_multiply_fusion
  1.4 0.1 copy.23
  1.5 0.1 eq.27
  1.6 0.1 eq.31
  1.8 0.1 convert_reduce_fusion
  1.9 1.2 %dynamic-slice = u32[1]{0:T(128)} dynamic-slice(u32[32]{0:T(128)} %constant.70, u32[]{:T(128)S(6)} %add.123), dynamic_slice_sizes={1} | dynamic-slice | bytes 12
  3.8 0.2 dynamic-update-slice
  4.1 8.7 %all-reduce = s32[256]{0:T(256)S(1)} all-reduce(s32[256]{0:T(256)S(1)} %dynamic-update-slice), channel_id=2, replica_groups=mesh['groups'=2,'expert'=16] {'expert'}, use_global_device_ids=true, to_apply=%add | all-reduce | flops 256 | bytes 2048
  12.8 0.1 reshape.211
  12.9 0.6 reduce-window.6
  13.5 0.2 slice_reduce_fusion
  13.7 0.1 copy.28
  13.8 0.1 mul.88
  14.0 0.1 multiply_reduce_fusion.1
  14.1 0.7 select_reduce_fusion.1
  14.8 0.0 copy-done
  14.9 3.7 %scatter_custom_fusion = bf16[512,1024]{1,0:T(8,128)(2,1)S(1)} fusion(s32[256]{0:T(256)S(1)} %bitcast.43, bf16[128,1024]{1,0:T(8,128)(2,1)S(1)} %copy-done, s32[1024]{0:T(1024)S(1)} %pad_clamp_fusion.1, bf16[]{:T(256)} %constant.56.clone.1), kind=kCustom, calls=%fused_computation.18 | custom fusion | bytes 1048578 | tf_op jit(solution)/shard_map/scatter | solution.py:66
  18.6 32.1 %all_to_all.10 = bf16[16,32,1024]{2,1,0:T(8,128)(2,1)S(1)} all-to-all(bf16[16,32,1024]{2,1,0:T(8,128)(2,1)S(1)} %bitcast.36), channel_id=1, replica_groups=mesh['groups'=2,'expert'=16] {'expert'}, dimensions={0} | all-to-all | bytes 2097152 | tf_op jit(solution)/shard_map/all_to_all | solution.py:69
  50.7 0.0 copy-start.1
  50.7 9.0 %fusion.14 = bf16[512,1024]{1,0:T(8,128)(2,1)} fusion(bf16[1,2048,1024]{2,1,0:T(8,128)(2,1)} %param.13, bf16[512,1024]{1,0:T(8,128)(2,1)S(1)} %bitcast.37, bf16[1,1024,2048]{2,1,0:T(8,128)(2,1)} %param.12), kind=kOutput, calls=%fused_computation.16 | convolution fusion | flops 4304928768 | bytes 10485760 | tf_op jit(solution)/shard_map/dot_general | solution.py:14
  59.8 4.3 %all-to-all-start.1 = ((bf16[16,32,1024]{2,1,0:T(8,128)(2,1)}), bf16[16,32,1024]{2,1,0:T(8,128)(2,1)S(1)}, u32[]{:S(2)}, u32[]{:S(2)}) async-start(bf16[16,32,1024]{2,1,0:T(8,128)(2,1)} %bitcast.11), calls=%async_computation.1 | async-start | bytes 2097152 | tf_op jit(solution)/shard_map/all_to_all | solution.py:70
  64.0 0.2 lt.73
  64.2 0.1 copy.26
  64.3 0.0 copy-done.1
  64.3 0.1 copy.27
  64.5 24.5 %all-to-all-done.1 = bf16[16,32,1024]{2,1,0:T(8,128)(2,1)S(1)} async-done(((bf16[16,32,1024]{2,1,0:T(8,128)(2,1)}), bf16[16,32,1024]{2,1,0:T(8,128)(2,1)S(1)}, u32[]{:S(2)}, u32[]{:S(2)}) %all-to-all-start.1) | async-done | bytes 1048608 | tf_op jit(solution)/shard_map/all_to_all | solution.py:70
  88.9 1.2 %gather_fusion = bf16[256,1024]{1,0:T(8,128)(2,1)S(1)} fusion(bf16[512,1024]{1,0:T(8,128)(2,1)S(1)} %bitcast.35, s32[1024]{0:T(1024)S(1)} %pad_clamp_fusion), kind=kCustom, calls=%fused_computation.1 | custom fusion | bytes 1049600 | tf_op jit(solution)/shard_map/gather | solution.py:82
  90.1 0.7 reshape.186
  90.8 2.1 %multiply_reduce_fusion = bf16[128,1024]{1,0:T(8,128)(2,1)} fusion(f32[128,2,1024]{2,1,0:T(2,128)S(1)} %reshape.186, f32[128,2]{1,0:T(8,128)S(1)} %copy.27), kind=kLoop, calls=%fused_computation.17 | loop fusion | flops 393216 | bytes 1311744 | tf_op jit(solution)/shard_map/reduce_sum | solution.py:87
  (12 shorter events, 0.1 us)
Async XLA Ops:
  0.0 14.8 %copy-start = (bf16[128,1024]{1,0:T(8,128)(2,1)S(1)}, bf16[128,1024]{1,0:T(8,128)(2,1)}, u32[]{:S(2)}) copy-start(bf16[128,1024]{1,0:T(8,128)(2,1)} %param.7) | copy-start | bytes 786436
  50.7 13.6 %copy-start.1 = (s32[128,2]{0,1:T(2,128)S(1)}, s32[128,2]{0,1:T(2,128)}, u32[]{:S(2)}) copy-start(s32[128,2]{0,1:T(2,128)} %param.10) | copy-start | bytes 3076
  59.8 29.2 %all-to-all-start.1 = ((bf16[16,32,1024]{2,1,0:T(8,128)(2,1)}), bf16[16,32,1024]{2,1,0:T(8,128)(2,1)S(1)}, u32[]{:S(2)}, u32[]{:S(2)}) async-start(bf16[16,32,1024]{2,1,0:T(8,128)(2,1)} %bitcast.11), calls=%async_computation.1 | async-start | bytes 2097152 | tf_op jit(solution)/shard_map/all_to_all | solution.py:70
where the time goes:
time: 93.1 us; the launch traced here: 92.8 us
  blocking collectives  40.9 us (44%)
  waiting for transfers between devices  24.5 us (26%)
  matrix products  9.05 us (10%)
  local copies, waits for them, and re-layouts  8.28 us (9%)
  other arithmetic  5.12 us (5%)
  starting transfers between devices  4.27 us (5%)
    all_to_all x1, blocking collectives, shards(): lax.all_to_all(outgoing, 'expert', split_axis=0, concat_axis=0, tiled=True)  32.1 us
    all_to_all x1, waiting for transfers between devices, shards(): lax.all_to_all(expert_mlp(arrived.reshape(-1, feature_width), up_matrix,...  24.5 us
    dot_general x1, matrix products, expert_mlp(): jnp.dot(hidden, down_matrix, preferred_element_type=jnp.float32)  9.05 us
    unnamed x1, blocking collectives  8.74 us
    all_to_all x1, starting transfers between devices, shards(): lax.all_to_all(expert_mlp(arrived.reshape(-1, feature_width), up_matrix,...  4.27 us
    scatter x1, local copies, waits for them, and re-layouts, shards(): outgoing = outgoing.at[send_index].set(query_features[source_rows], mode=...  3.71 us
    reduce_sum x1, other arithmetic, shards(): jnp.sum(weighted.reshape(row_count, top_count, feature_width), axis=1)  2.08 us
  transfers between devices with their start and end apart: 1, of which 1 were waited for; matrix products, arithmetic and copies ran while one was open for 0% of the time, Pallas kernels for 0%

commit v1 on v0

v1 whole, which is shorter than its diff:
```python
import functools

import jax
import jax.numpy as jnp
from jax import lax
from jax.experimental import pallas as pl
from jax.experimental.pallas import tpu as pltpu
from jax.sharding import PartitionSpec as P

TASKS = 8
SHARED = 8
MESH = pl.DeviceIdType.MESH


def flip(a, b, n):
    total, bit = 0, 1
    while bit < n:
        x, y = (a // bit) % 2, (b // bit) % 2
        total = total + bit * (x + y - 2 * x * y)
        bit *= 2
    return total


def each(lo, hi, fn):
    if hi - lo <= 16:
        for d in range(lo, hi):
            fn(d)
    else:

        @pl.loop(lo, hi)
        def _(d):
            fn(d)


def kernel(
    n,
    slot,
    room_ref,
    label_ref,
    sel_ref,
    mix_ref,
    x_ref,
    w1_hbm,
    w2_hbm,
    out_ref,
    w1,
    w2,
    outgoing,
    inbox,
    hidden,
    results,
    returned,
    counts,
    w_sem,
    send_sem,
    recv_sem,
    rsend_sem,
    rrecv_sem,
    csend_sem,
    crecv_sem,
):
    me = lax.axis_index("expert")
    group = lax.axis_index("groups")
    half = n // 2
    rows, width = x_ref.shape
    span = half * slot
    copies, task_width = n // (2 * SHARED), n // (2 * TASKS)

    load1 = pltpu.make_async_copy(w1_hbm.at[0], w1, w_sem.at[0])
    load2 = pltpu.make_async_copy(w2_hbm.at[0], w2, w_sem.at[1])
    load1.start()
    load2.start()

    barrier = pltpu.get_barrier_semaphore()

    def peer(d):
        return (group, flip(me, d, n))

    each(
        1,
        n,
        lambda d: pl.semaphore_signal(
            barrier, inc=1, device_id=peer(d), device_id_type=MESH
        ),
    )

    lane = lax.broadcasted_iota(jnp.int32, (1, rows), 1)
    task_id = SHARED * copies + label_ref[...] * task_width + sel_ref[0:1, :] - SHARED
    shared_id = sel_ref[1:2, :] * copies + lane % copies
    expert = lax.broadcasted_iota(jnp.int32, (n, rows), 0)
    hot = (expert == task_id) | (expert == shared_id)
    hot_f = hot.astype(jnp.float32)
    earlier = (
        lax.broadcasted_iota(jnp.int32, (rows, rows), 0)
        < lax.broadcasted_iota(jnp.int32, (rows, rows), 1)
    ).astype(jnp.float32)
    before = jnp.dot(
        hot_f.astype(jnp.bfloat16),
        earlier.astype(jnp.bfloat16),
        preferred_element_type=jnp.float32,
    )
    task_hot = (expert == task_id).astype(jnp.float32)
    shared_hot = (expert == shared_id).astype(jnp.float32)
    task_rank = jnp.sum(before * task_hot, axis=0, keepdims=True)
    shared_rank = jnp.sum(before * shared_hot, axis=0, keepdims=True)
    counts[0] = jnp.broadcast_to(jnp.sum(hot_f, axis=1, keepdims=True), (n, 128))

    task_slot = (task_id ^ me) * slot + task_rank.astype(jnp.int32)
    shared_slot = (shared_id ^ me) * slot + shared_rank.astype(jnp.int32)
    task_near = task_slot < span
    near_slot = jnp.where(task_near, task_slot, shared_slot)
    far_slot = jnp.where(task_near, shared_slot, task_slot) - span
    slot_row = lax.broadcasted_iota(jnp.int32, (span, rows), 0)

    def pack(slots):
        chosen = (slot_row == slots).astype(jnp.float32).astype(jnp.bfloat16)
        return jnp.dot(chosen, x_ref[...], preferred_element_type=jnp.float32).astype(
            jnp.bfloat16
        )

    def piece(ref, d):
        if isinstance(d, int):
            return ref.at[pl.ds(d * slot, slot)]
        return ref.at[pl.ds(pl.multiple_of(d * slot, slot), slot)]

    def dispatch(d):
        return pltpu.make_async_remote_copy(
            src_ref=piece(outgoing, d),
            dst_ref=piece(inbox, d),
            send_sem=send_sem.at[d],
            recv_sem=recv_sem.at[d],
            device_id=peer(d),
            device_id_type=MESH,
        )

    def answer(d):
        return pltpu.make_async_remote_copy(
            src_ref=piece(results, d),
            dst_ref=piece(returned, d),
            send_sem=rsend_sem.at[d],
            recv_sem=rrecv_sem.at[d],
            device_id=peer(d),
            device_id_type=MESH,
        )

    def tally(d):
        return pltpu.make_async_remote_copy(
            src_ref=counts.at[0],
            dst_ref=counts.at[d],
            send_sem=csend_sem.at[d],
            recv_sem=crecv_sem.at[d],
            device_id=peer(d),
            device_id_type=MESH,
        )

    outgoing[pl.ds(span, span)] = pack(far_slot)
    near_pack = pack(near_slot)
    outgoing[pl.ds(0, span)] = near_pack
    inbox[pl.ds(0, slot)] = near_pack[:slot]

    pl.semaphore_wait(barrier, n - 1)
    each(1, n, lambda d: dispatch(d).start())
    each(1, n, lambda d: tally(d).start())

    hid = w1.shape[1]
    tile = min(512, hid)
    out_tile = min(512, width)

    def mlp(first, size):
        @pl.loop(0, hid // tile)
        def _(t):
            cols = pl.ds(pl.multiple_of(t * tile, tile), tile)
            h = jnp.dot(
                inbox[pl.ds(first, size)],
                w1[:, cols],
                preferred_element_type=jnp.float32,
            )
            hidden[pl.ds(0, size), cols] = jax.nn.gelu(h).astype(jnp.bfloat16)

        @pl.loop(0, width // out_tile)
        def _(t):
            cols = pl.ds(pl.multiple_of(t * out_tile, out_tile), out_tile)
            y = jnp.dot(
                hidden[pl.ds(0, size)], w2[:, cols], preferred_element_type=jnp.float32
            )
            results[pl.ds(first, size), cols] = y.astype(jnp.bfloat16)

    load1.wait()
    load2.wait()
    each(1, half, lambda d: dispatch(d).wait_recv())
    mlp(0, span)
    each(1, half, lambda d: answer(d).start())
    returned[pl.ds(0, slot)] = results[pl.ds(0, slot)]

    quarter = half // 2
    for lo in (half, half + quarter):
        each(lo, lo + quarter, lambda d: dispatch(d).wait_recv())
        mlp(lo * slot, quarter * slot)
        each(lo, lo + quarter, lambda d: answer(d).start())

    each(1, n, lambda d: tally(d).wait_recv())

    offset = jnp.zeros((n, 128), jnp.float32)
    for d in range(1, n):
        source = flip(me, d, n)
        offset = offset + counts[d] * jnp.where(source < me, 1.0, 0.0)
    offset = offset[:, :1]
    arrival_task = task_rank + jnp.sum(task_hot * offset, axis=0, keepdims=True)
    arrival_shared = shared_rank + jnp.sum(shared_hot * offset, axis=0, keepdims=True)
    room_task = jnp.zeros((1, rows), jnp.int32)
    room_shared = jnp.zeros((1, rows), jnp.int32)
    for e in range(n):
        size = room_ref[e]
        if e < half:
            room_shared = jnp.where(shared_id == e, size, room_shared)
        else:
            room_task = jnp.where(task_id == e, size, room_task)
    keep_task = (arrival_task < room_task.astype(jnp.float32)).astype(jnp.float32)
    keep_shared = (arrival_shared < room_shared.astype(jnp.float32)).astype(jnp.float32)
    mix = mix_ref[...].astype(jnp.float32)
    total = mix[0:1] + mix[1:2]
    task_weight = mix[0:1] / total * keep_task
    shared_weight = mix[1:2] / total * keep_shared
    near_weight = jnp.where(task_near, task_weight, shared_weight)
    far_weight = jnp.where(task_near, shared_weight, task_weight)

    def column(row):
        return jnp.broadcast_to(row, (128, rows)).T[:, :1]

    near_column = column(near_slot.astype(jnp.float32))
    far_column = column(far_slot.astype(jnp.float32))
    near_weight = column(near_weight)
    far_weight = column(far_weight)
    slot_lane = lax.broadcasted_iota(jnp.int32, (rows, span), 1).astype(jnp.float32)

    def pick(slots, first):
        chosen = (slot_lane == slots).astype(jnp.float32).astype(jnp.bfloat16)
        return jnp.dot(
            chosen, returned[pl.ds(first, span)], preferred_element_type=jnp.float32
        )

    each(1, half, lambda d: answer(d).wait_recv())
    near = pick(near_column, 0) * near_weight
    each(half, n, lambda d: answer(d).wait_recv())
    out_ref[...] = (near + pick(far_column, span) * far_weight).astype(jnp.bfloat16)

    def drain(d):
        dispatch(d).wait_send()
        answer(d).wait_send()
        tally(d).wait_send()

    each(1, n, drain)


def solution(mesh):
    n = mesh.shape["expert"]

    def shards(x, label, sel, mix, room, first, second):
        rows, width = x.shape
        hid = first.shape[2]
        slot = -(-(4 * rows // n) // 16) * 16
        flat = pltpu.VMEM((n * slot, width), jnp.bfloat16)
        vmem = pl.BlockSpec(memory_space=pltpu.VMEM)
        anywhere = pl.BlockSpec(memory_space=pl.ANY)
        return pl.pallas_call(
            functools.partial(kernel, n, slot),
            out_shape=jax.ShapeDtypeStruct((rows, width), jnp.bfloat16),
            in_specs=[pl.BlockSpec(memory_space=pltpu.SMEM)]
            + [vmem] * 4
            + [anywhere] * 2,
            out_specs=vmem,
            scratch_shapes=[
                pltpu.VMEM(first.shape[1:], jnp.bfloat16),
                pltpu.VMEM(second.shape[1:], jnp.bfloat16),
                flat,
                flat,
                pltpu.VMEM((n * slot // 2, hid), jnp.bfloat16),
                flat,
                flat,
                pltpu.VMEM((n, n, 128), jnp.float32),
                pltpu.SemaphoreType.DMA((2,)),
            ]
            + [pltpu.SemaphoreType.DMA((n,))] * 6,
            compiler_params=pltpu.CompilerParams(
                collective_id=0, has_side_effects=True
            ),
        )(room, label.reshape(1, rows), sel.T, mix.T, x, first, second)

    in_specs = (
        P(("groups", "expert"), None),
        P(("groups", "expert")),
        P(("groups", "expert"), None),
        P(("groups", "expert"), None),
        P(),
        P("expert", None, None),
        P("expert", None, None),
    )
    return jax.shard_map(
        shards,
        mesh=mesh,
        in_specs=in_specs,
        out_specs=P(("groups", "expert"), None),
        check_vma=False,
    )
```

time: 93.1 us -> 58.5 us (0.63)
  Pallas kernels: 0 us -> 55.9 us
  blocking collectives: 40.9 us -> 0 us
  waiting for transfers between devices: 24.5 us -> 0 us
  matrix products: 9.05 us -> 0 us
  local copies, waits for them, and re-layouts: 8.28 us -> 1.67 us
  other arithmetic: 5.12 us -> 0 us
  starting transfers between devices: 4.27 us -> 0 us
    pallas_call x0 -> x1, Pallas kernels: none -> 55.9 us  [shards(): pl.pallas_call(functools.partial(kernel, n, slot), out_shape=jax.ShapeDty...]
    all_to_all x1 -> x0, blocking collectives: 32.1 us -> none  [shards(): lax.all_to_all(outgoing, 'expert', split_axis=0, concat_axis=0, tiled=True)]
    all_to_all x1 -> x0, waiting for transfers between devices: 24.5 us -> none  [shards(): lax.all_to_all(expert_mlp(arrived.reshape(-1, feature_width), up_matrix,...]
    dot_general x1 -> x0, matrix products: 9.05 us -> none  [expert_mlp(): jnp.dot(hidden, down_matrix, preferred_element_type=jnp.float32)]
    unnamed x1 -> x0, blocking collectives: 8.74 us -> none
    all_to_all x1 -> x0, starting transfers between devices: 4.27 us -> none  [shards(): lax.all_to_all(expert_mlp(arrived.reshape(-1, feature_width), up_matrix,...]
    scatter x1 -> x0, local copies, waits for them, and re-layouts: 3.71 us -> none  [shards(): outgoing = outgoing.at[send_index].set(query_features[source_rows], mode=...]
    reduce_sum x5 -> x0, other arithmetic: 3.06 us -> none  [the longest x1 2.08 us: shards(): jnp.sum(weighted.reshape(row_count, top_count, feature_width), axis=1)]
  transfers between devices with their start and end apart: 1 -> 0, of which waited for: 1 -> 0; matrix products, arithmetic and copies ran while one was open for 0% -> 0% of each run, Pallas kernels for 0% -> 0%
where the time goes in v1:
time: 58.5 us; the launch traced here: 57.6 us
  Pallas kernels  55.9 us (96%)
  local copies, waits for them, and re-layouts  1.67 us (3%)
    pallas_call x1, Pallas kernels, shards(): pl.pallas_call(functools.partial(kernel, n, slot), out_shape=jax.ShapeDty...  55.9 us
    unnamed x1, local copies, waits for them, and re-layouts  1.67 us

profile of v1, /device:TPU:9, one launch (start us, length us, event | category | flops | bytes accessed | tf_op | source)
XLA Modules:
  0.0 57.6 jit_solution(2613174657225750882)
XLA Ops:
  0.0 55.9 %shard_map.73 = bf16[128,1024]{1,0:T(8,128)(2,1)} custom-call(s32[16]{0:T(128)} %room_ref.1, s32[1,128]{1,0:T(1,128)} %bitcast.5, s32[2,128]{1,0:T(2,128)} %bitcast.3, s32[2,128]{1,0:T(2,128)} %bitcast.4, bf16[128,1024]{1,0:T(8,128)(2,1)} %x_ref.1, bf16[1,1024,2048]{2,1,0:T(8,128)(2,1)} %w1_hbm.1, bf16[1,2048,1024]{2,1,0:T(8,128)(2,1)} %w2_hbm.1), custom_call_target="tpu_custom_call" | custom-call | tf_op jit(solution)/shard_map/pallas_call | solution.py:265
  55.9 1.7 %copy.9 = bf16[128,1024]{1,0:T(8,128)(2,1)} copy(bf16[128,1024]{1,0:T(8,128)(2,1)} %shard_map.73) | data formatting | bytes 524288

commit v2 on v1

v2 whole, which is shorter than its diff:
```python
import functools

import jax
import jax.numpy as jnp
from jax import lax
from jax.experimental import pallas as pl
from jax.experimental.pallas import tpu as pltpu
from jax.sharding import PartitionSpec as P

TASKS = 8
SHARED = 8
MESH = pl.DeviceIdType.MESH
CHUNKS = 4


def flip(a, b, n):
    total, bit = 0, 1
    while bit < n:
        x, y = (a // bit) % 2, (b // bit) % 2
        total = total + bit * (x + y - 2 * x * y)
        bit *= 2
    return total


def each(lo, hi, fn):
    if hi - lo <= 16:
        for d in range(lo, hi):
            fn(d)
    else:

        @pl.loop(lo, hi)
        def _(d):
            fn(d)


def kernel(
    n,
    slot,
    chunks,
    room_ref,
    label_ref,
    sel_ref,
    mix_ref,
    x_ref,
    w1_hbm,
    w2_hbm,
    out_ref,
    w1,
    w2,
    guests,
    outgoing,
    inbox,
    hidden,
    results,
    returned,
    home_out,
    home_in,
    partial,
    counts,
    route,
    w_sem,
    dense_sem,
    back_sem,
    route_sem,
    tally_send,
    tally_recv,
    near_send,
    near_recv,
    far_send,
    far_recv,
    near_rsend,
    near_rrecv,
    far_rsend,
    far_rrecv,
):
    me = lax.axis_index("expert")
    group = lax.axis_index("groups")
    half = n // 2
    rows, width = x_ref.shape
    span = half * slot
    part = width // chunks
    hid = w1.shape[1]
    padded = counts.shape[2]
    copies, task_width = n // (2 * SHARED), n // (2 * TASKS)

    load1 = pltpu.make_async_copy(w1_hbm.at[0], w1, w_sem.at[0])
    load2 = pltpu.make_async_copy(w2_hbm.at[0], w2, w_sem.at[1])
    load1.start()
    load2.start()

    barrier = pltpu.get_barrier_semaphore()

    def peer(d):
        return (group, flip(me, d, n))

    each(
        1,
        n,
        lambda d: pl.semaphore_signal(
            barrier, inc=1, device_id=peer(d), device_id_type=MESH
        ),
    )

    def remote(src, dst, send, recv, d):
        return pltpu.make_async_remote_copy(
            src_ref=src,
            dst_ref=dst,
            send_sem=send,
            recv_sem=recv,
            device_id=peer(d),
            device_id_type=MESH,
        )

    def block(first, d, k=None):
        start = first + d * slot
        if not isinstance(d, int):
            start = pl.multiple_of(start, slot)
        if k is None:
            return (pl.ds(start, slot), slice(None))
        return (pl.ds(start, slot), pl.ds(k * part, part))

    def columns(k):
        return (slice(None), pl.ds(k * part, part))

    def tally(d):
        return remote(
            counts.at[0], counts.at[d], tally_send.at[d], tally_recv.at[d], d
        )

    def plan():
        return remote(route.at[0], route.at[1], route_sem.at[0], route_sem.at[1], half)

    def dense(k):
        return remote(
            x_ref.at[columns(k)],
            guests.at[columns(k)],
            dense_sem.at[0, k],
            dense_sem.at[1, k],
            half,
        )

    def back(k):
        return remote(
            home_out.at[columns(k)],
            home_in.at[columns(k)],
            back_sem.at[0, k],
            back_sem.at[1, k],
            half,
        )

    def near_dispatch(d):
        at = block(0, d)
        return remote(outgoing.at[at], inbox.at[at], near_send.at[d], near_recv.at[d], d)

    def far_dispatch(d, k):
        at = block(span, d, k)
        return remote(
            outgoing.at[at], inbox.at[at], far_send.at[d, k], far_recv.at[d, k], d
        )

    def near_answer(d):
        at = block(0, d)
        return remote(
            results.at[at], returned.at[at], near_rsend.at[d], near_rrecv.at[d], d
        )

    def far_answer(d, k):
        at = block(span, d, k)
        return remote(
            results.at[at], returned.at[at], far_rsend.at[d, k], far_rrecv.at[d, k], d
        )

    lane = lax.broadcasted_iota(jnp.int32, (1, rows), 1)
    task_id = SHARED * copies + label_ref[...] * task_width + sel_ref[0:1, :] - SHARED
    shared_id = sel_ref[1:2, :] * copies + lane % copies
    expert = lax.broadcasted_iota(jnp.int32, (padded, rows), 0)
    task_hot = (expert == task_id).astype(jnp.float32)
    shared_hot = (expert == shared_id).astype(jnp.float32)
    hot = (task_hot + shared_hot).astype(jnp.bfloat16)
    earlier = (
        lax.broadcasted_iota(jnp.int32, (rows, rows), 0)
        < lax.broadcasted_iota(jnp.int32, (rows, rows), 1)
    ).astype(jnp.float32)
    before = jnp.dot(
        hot, earlier.astype(jnp.bfloat16), preferred_element_type=jnp.float32
    )
    task_rank = jnp.sum(before * task_hot, axis=0, keepdims=True)
    shared_rank = jnp.sum(before * shared_hot, axis=0, keepdims=True)
    counts[0] = lax.dot_general(
        jnp.ones((8, rows), jnp.bfloat16),
        hot,
        (((1,), (1,)), ((), ())),
        preferred_element_type=jnp.float32,
    )[:1]

    task_slot = (task_id ^ me) * slot + task_rank.astype(jnp.int32)
    shared_slot = (shared_id ^ me) * slot + shared_rank.astype(jnp.int32)
    task_near = task_slot < span
    near_slot = jnp.where(task_near, task_slot, shared_slot)
    far_slot = jnp.where(task_near, shared_slot, task_slot) - span
    route[0] = far_slot
    slot_row = lax.broadcasted_iota(jnp.int32, (span, rows), 0)

    def choice(slots):
        return (slot_row == slots).astype(jnp.float32).astype(jnp.bfloat16)

    def pack(chosen, block_rows):
        return jnp.dot(chosen, block_rows, preferred_element_type=jnp.float32).astype(
            jnp.bfloat16
        )

    near_pack = pack(choice(near_slot), x_ref[...])
    outgoing[pl.ds(0, span)] = near_pack
    inbox[pl.ds(0, slot)] = near_pack[:slot]

    pl.semaphore_wait(barrier, n - 1)
    plan().start()
    for k in range(chunks):
        dense(k).start()
    each(1, n, lambda d: tally(d).start())
    each(1, half, lambda d: near_dispatch(d).start())

    plan().wait_recv()
    guest_slot = route[1]
    guest_choice = choice(guest_slot)
    for k in range(chunks):
        dense(k).wait_recv()
        packed = pack(guest_choice, guests[columns(k)])
        outgoing[pl.ds(span, span), pl.ds(k * part, part)] = packed
        inbox[pl.ds(span, slot), pl.ds(k * part, part)] = packed[:slot]
        each(1, half, lambda d: far_dispatch(d, k).start())

    tile = min(512, hid)

    def expand(first):
        @pl.loop(0, hid // tile)
        def _(t):
            cols = pl.ds(pl.multiple_of(t * tile, tile), tile)
            h = jnp.dot(
                inbox[pl.ds(first, span)],
                w1[:, cols],
                preferred_element_type=jnp.float32,
            )
            hidden[:, cols] = jax.nn.gelu(h).astype(jnp.bfloat16)

    def shrink(first, cols):
        y = jnp.dot(hidden[...], w2[:, cols], preferred_element_type=jnp.float32)
        results[pl.ds(first, span), cols] = y.astype(jnp.bfloat16)

    load1.wait()
    load2.wait()
    each(1, half, lambda d: near_dispatch(d).wait_recv())
    expand(0)

    out_tile = min(512, width)

    @pl.loop(0, width // out_tile)
    def _(t):
        shrink(0, pl.ds(pl.multiple_of(t * out_tile, out_tile), out_tile))

    each(1, half, lambda d: near_answer(d).start())
    returned[pl.ds(0, slot)] = results[pl.ds(0, slot)]

    for k in range(chunks):
        each(1, half, lambda d: far_dispatch(d, k).wait_recv())
    expand(span)
    for k in range(chunks):
        shrink(span, pl.ds(k * part, part))
        each(1, half, lambda d: far_answer(d, k).start())
        own = (pl.ds(span, slot), pl.ds(k * part, part))
        returned[own] = results[own]

    each(1, n, lambda d: tally(d).wait_recv())

    def column(row):
        return jnp.broadcast_to(row, (128, row.shape[1])).T[:, :1]

    offset = jnp.zeros((1, padded), jnp.float32)
    for d in range(1, n):
        offset = offset + counts[d] * jnp.where(flip(me, d, n) < me, 1.0, 0.0)
    offset = column(offset)
    arrival_task = task_rank + jnp.sum(task_hot * offset, axis=0, keepdims=True)
    arrival_shared = shared_rank + jnp.sum(shared_hot * offset, axis=0, keepdims=True)
    room_task = jnp.zeros((1, rows), jnp.int32)
    room_shared = jnp.zeros((1, rows), jnp.int32)
    for e in range(n):
        size = room_ref[e]
        if e < half:
            room_shared = jnp.where(shared_id == e, size, room_shared)
        else:
            room_task = jnp.where(task_id == e, size, room_task)
    keep_task = (arrival_task < room_task.astype(jnp.float32)).astype(jnp.float32)
    keep_shared = (arrival_shared < room_shared.astype(jnp.float32)).astype(jnp.float32)
    mix = mix_ref[...].astype(jnp.float32)
    total = mix[0:1] + mix[1:2]
    task_weight = mix[0:1] / total * keep_task
    shared_weight = mix[1:2] / total * keep_shared
    near_weight = column(jnp.where(task_near, task_weight, shared_weight))
    far_weight = column(jnp.where(task_near, shared_weight, task_weight))
    slot_lane = lax.broadcasted_iota(jnp.int32, (rows, span), 1).astype(jnp.float32)

    def reader(slots):
        slots = column(slots.astype(jnp.float32))
        return (slot_lane == slots).astype(jnp.float32).astype(jnp.bfloat16)

    near_reader = reader(near_slot)
    guest_reader = reader(guest_slot)

    each(1, half, lambda d: near_answer(d).wait_recv())
    partial[...] = (
        jnp.dot(
            near_reader, returned[pl.ds(0, span)], preferred_element_type=jnp.float32
        )
        * near_weight
    )

    for k in range(chunks):
        each(1, half, lambda d: far_answer(d, k).wait_recv())
        home_out[columns(k)] = pack(
            guest_reader, returned[pl.ds(span, span), pl.ds(k * part, part)]
        )
        back(k).start()

    for k in range(chunks):
        back(k).wait_recv()
        out_ref[columns(k)] = (
            partial[columns(k)] + home_in[columns(k)].astype(jnp.float32) * far_weight
        ).astype(jnp.bfloat16)

    plan().wait_send()
    each(1, n, lambda d: tally(d).wait_send())
    for k in range(chunks):
        dense(k).wait_send()
        back(k).wait_send()

    def drain(d):
        near_dispatch(d).wait_send()
        near_answer(d).wait_send()
        for k in range(chunks):
            far_dispatch(d, k).wait_send()
            far_answer(d, k).wait_send()

    each(1, half, drain)


def solution(mesh):
    n = mesh.shape["expert"]

    def shards(x, label, sel, mix, room, first, second):
        rows, width = x.shape
        hid = first.shape[2]
        slot = -(-(4 * rows // n) // 16) * 16
        chunks = CHUNKS
        half = n // 2
        padded = -(-n // 128) * 128
        flat = pltpu.VMEM((n * slot, width), jnp.bfloat16)
        plain = pltpu.VMEM((rows, width), jnp.bfloat16)
        vmem = pl.BlockSpec(memory_space=pltpu.VMEM)
        anywhere = pl.BlockSpec(memory_space=pl.ANY)
        dma = pltpu.SemaphoreType.DMA
        return pl.pallas_call(
            functools.partial(kernel, n, slot, chunks),
            out_shape=jax.ShapeDtypeStruct((rows, width), jnp.bfloat16),
            in_specs=[pl.BlockSpec(memory_space=pltpu.SMEM)]
            + [vmem] * 4
            + [anywhere] * 2,
            out_specs=vmem,
            scratch_shapes=[
                pltpu.VMEM(first.shape[1:], jnp.bfloat16),
                pltpu.VMEM(second.shape[1:], jnp.bfloat16),
                plain,
                flat,
                flat,
                pltpu.VMEM((half * slot, hid), jnp.bfloat16),
                flat,
                flat,
                plain,
                plain,
                pltpu.VMEM((rows, width), jnp.float32),
                pltpu.VMEM((n, 1, padded), jnp.float32),
                pltpu.VMEM((2, 1, rows), jnp.int32),
                dma((2,)),
                dma((2, chunks)),
                dma((2, chunks)),
                dma((2,)),
                dma((n,)),
                dma((n,)),
                dma((half,)),
                dma((half,)),
                dma((half, chunks)),
                dma((half, chunks)),
                dma((half,)),
                dma((half,)),
                dma((half, chunks)),
                dma((half, chunks)),
            ],
            compiler_params=pltpu.CompilerParams(
                collective_id=0, has_side_effects=True
            ),
        )(room, label.reshape(1, rows), sel.T, mix.T, x, first, second)

    in_specs = (
        P(("groups", "expert"), None),
        P(("groups", "expert")),
        P(("groups", "expert"), None),
        P(("groups", "expert"), None),
        P(),
        P("expert", None, None),
        P("expert", None, None),
    )
    return jax.shard_map(
        shards,
        mesh=mesh,
        in_specs=in_specs,
        out_specs=P(("groups", "expert"), None),
        check_vma=False,
    )
```

time: 58.5 us -> 51.8 us (0.89)
  the two profiles are of different devices: /device:TPU:9 before, /device:TPU:0 now
where the time goes in v2:
time: 51.8 us; the launch traced here: 51.6 us
  Pallas kernels  50 us (97%)
  local copies, waits for them, and re-layouts  1.67 us (3%)
    pallas_call x1, Pallas kernels, shards(): pl.pallas_call(functools.partial(kernel, n, slot, chunks), out_shape=jax....  50 us
    unnamed x1, local copies, waits for them, and re-layouts  1.67 us

profile of v2, /device:TPU:0, one launch (start us, length us, event | category | flops | bytes accessed | tf_op | source)
XLA Modules:
  0.0 51.6 jit_solution(4690028285739517586)
XLA Ops:
  0.0 50.0 %shard_map.73 = bf16[128,1024]{1,0:T(8,128)(2,1)} custom-call(s32[16]{0:T(128)} %room_ref.1, s32[1,128]{1,0:T(1,128)} %bitcast.5, s32[2,128]{1,0:T(2,128)} %bitcast.3, s32[2,128]{1,0:T(2,128)} %bitcast.4, bf16[128,1024]{1,0:T(8,128)(2,1)} %x_ref.1, bf16[1,1024,2048]{2,1,0:T(8,128)(2,1)} %w1_hbm.1, bf16[1,2048,1024]{2,1,0:T(8,128)(2,1)} %w2_hbm.1), custom_call_target="tpu_custom_call" | custom-call | tf_op jit(solution)/shard_map/pallas_call | solution.py:361
  50.0 1.7 %copy.9 = bf16[128,1024]{1,0:T(8,128)(2,1)} copy(bf16[128,1024]{1,0:T(8,128)(2,1)} %shard_map.73) | data formatting | bytes 524288
